TPU v7x, 32 devices: a whole 2x2x4 slice. The times are simulated.
32 devices in a mesh: seq: 4 (over z), uly: 4 (over y, x), rep: 2 (over core).
Axes of the slice: x: 2, y: 2, z: 4, core: 2. Of those that a mesh axis runs over, the one named last changes fastest.
Arguments:
- queries: bfloat16 [4096, 2048], P(('rep', 'seq', 'uly')), parts along dimension 0, may hold values from -6 to 6
- keys: bfloat16 [4096, 2048], P(('rep', 'seq', 'uly')), parts along dimension 0, may hold values from -6 to 6
- values: bfloat16 [4096, 2048], P(('rep', 'seq', 'uly')), parts along dimension 0, may hold values from -6 to 6
- past_outputs: bfloat16 [2, 4096, 2048], P(None, ('rep', 'seq', 'uly')), parts along dimension 1, may hold values from -6 to 6
- dwa_slot: int32 [2], replicated, may hold values from 0 to 63
- dwa_table: float32 [2, 64], replicated, may hold values from 0.1 to 0.6
Outputs:
- mixed: bfloat16 [4096, 2048], P(('rep', 'seq', 'uly')), parts along dimension 0
There are 2 independent parts, one for each index of `rep`. A program takes and returns all parts, laid end to end along the dimension named above; an argument that names none is the same for every part. Nothing has to cross between parts.
All inputs are finite; a program needn't handle non-finite values.
Results may differ from a plain program's by a relative error of at most 0.0034.
Values may be sent and summed in bfloat16 or wider, within the bound.
A program may use at most 64 MiB of HBM per device.

v0:
```python
import jax
import jax.numpy as jnp
from jax import lax
from jax.sharding import PartitionSpec as P

HEAD_DIM = 128


def from_behind(block, axis, distance):
    devices = range(lax.axis_size(axis))
    route = [(i - distance, i) for i in devices if i - distance in devices]
    return lax.ppermute(block, axis, route)


def block_update(state, query_heads, key_heads, value_heads, allowed):
    running, total, accumulated = state
    scores = jnp.einsum("qhd,khd->hqk", query_heads, key_heads, preferred_element_type=jnp.float32)
    scores = scores * (1.0 / HEAD_DIM**0.5)
    scores = jnp.where(allowed, scores, -jnp.inf)
    new_max = jnp.maximum(running, jnp.max(scores, axis=2))
    factor = jnp.exp(running - new_max)
    prob = jnp.exp(scores - new_max[:, :, None])
    total = total * factor + jnp.sum(prob, axis=2)
    weights = prob.astype(jnp.bfloat16)
    update = jnp.einsum("hqk,khd->qhd", weights, value_heads, preferred_element_type=jnp.float32)
    accumulated = accumulated * jnp.transpose(factor)[:, :, None] + update
    return (new_max, total, accumulated)


def shards(queries, keys, values, past_outputs, dwa_slot, dwa_table):
    n_uly = lax.axis_size("uly")
    n_seq = lax.axis_size("seq")
    span_size = min(4, n_seq)
    features = queries.shape[1]
    local_heads = features // n_uly // HEAD_DIM
    query_rows, key_rows, value_rows = (
        lax.all_to_all(queries, "uly", split_axis=1, concat_axis=0, tiled=True),
        lax.all_to_all(keys, "uly", split_axis=1, concat_axis=0, tiled=True),
        lax.all_to_all(values, "uly", split_axis=1, concat_axis=0, tiled=True),
    )
    row_count = query_rows.shape[0]
    split_shape = (row_count, local_heads, HEAD_DIM)
    query_heads = query_rows.reshape(split_shape)
    table_index = jnp.arange(dwa_table.shape[1])
    onehot = (dwa_slot[:, None] == table_index[None, :]).astype(jnp.float32)
    coefs = jnp.dot(onehot, jnp.transpose(dwa_table), precision=lax.Precision.HIGHEST)
    layer_in = jnp.zeros(queries.shape, jnp.float32)
    extra = jnp.zeros(queries.shape, jnp.float32)
    for index in range(past_outputs.shape[0]):
        stored = past_outputs[index].astype(jnp.float32)
        layer_in = layer_in + coefs[index, 0] * stored
        extra = extra + coefs[index, 1] * stored
    running = jnp.full((local_heads, row_count), -jnp.inf, jnp.float32)
    total = jnp.zeros((local_heads, row_count), jnp.float32)
    accumulated = jnp.zeros(split_shape, jnp.float32)
    state = (running, total, accumulated)
    causal = (jnp.arange(row_count)[:, None] >= jnp.arange(row_count)[None, :])[None, :, :]
    state = block_update(
        state, query_heads, key_rows.reshape(split_shape), value_rows.reshape(split_shape), causal
    )
    position = lax.axis_index("seq")
    current = (key_rows, value_rows)
    for offset in range(1, span_size):
        current = from_behind((current[0], current[1]), "seq", 1)
        far_keys = current[0].reshape(split_shape)
        far_values = current[1].reshape(split_shape)

        def take_block(carry, far_keys=far_keys, far_values=far_values):
            return block_update(carry, query_heads, far_keys, far_values, True)

        def keep_block(carry):
            return carry

        state = lax.cond(position >= offset, take_block, keep_block, state)
    running, total, accumulated = state
    attended = accumulated / jnp.transpose(total)[:, :, None]
    attended = attended.astype(jnp.bfloat16).reshape(row_count, local_heads * HEAD_DIM)
    returned = lax.all_to_all(attended, "uly", split_axis=0, concat_axis=1, tiled=True)
    hidden = layer_in + returned.astype(jnp.float32)
    return (hidden + extra).astype(jnp.bfloat16)


def solution(mesh):
    return jax.shard_map(
        shards,
        mesh=mesh,
        in_specs=(
            P(("rep", "seq", "uly"), None),
            P(("rep", "seq", "uly"), None),
            P(("rep", "seq", "uly"), None),
            P(None, ("rep", "seq", "uly"), None),
            P(),
            P(),
        ),
        out_specs=P(("rep", "seq", "uly"), None),
        check_vma=False,
    )
```

profile of v0, /device:TPU:24, one launch (start us, length us, event | category | flops | bytes accessed | tf_op | source)
XLA Modules:
  0.0 108.4 jit_solution(13092285454462107051)
XLA Ops:
  0.0 1.9 %copy.128 = bf16[16,4,8,512]{3,2,0,1:T(8,128)(2,1)} copy(bf16[16,4,8,512]{3,2,1,0:T(8,128)(2,1)} %bitcast.102) | data formatting | bytes 1048576 | tf_op jit(solution)/shard_map/all_to_all | solution.py:38
  1.9 3.7 %all-to-all-start.1 = ((bf16[128,4,512]{2,0,1:T(8,128)(2,1)}), bf16[128,4,512]{2,0,1:T(8,128)(2,1)S(1)}, u32[]{:S(2)}, u32[]{:S(2)}) async-start(bf16[128,4,512]{2,0,1:T(8,128)(2,1)} %bitcast.95), calls=%async_computation.1 | async-start | bytes 1048576 | tf_op jit(solution)/shard_map/all_to_all | solution.py:38
  5.7 1.9 %copy.127 = bf16[16,4,8,512]{3,2,0,1:T(8,128)(2,1)} copy(bf16[16,4,8,512]{3,2,1,0:T(8,128)(2,1)} %bitcast.103) | data formatting | bytes 1048576 | tf_op jit(solution)/shard_map/all_to_all | solution.py:39
  7.5 6.1 %all-to-all-done.1 = bf16[128,4,512]{2,0,1:T(8,128)(2,1)S(1)} async-done(((bf16[128,4,512]{2,0,1:T(8,128)(2,1)}), bf16[128,4,512]{2,0,1:T(8,128)(2,1)S(1)}, u32[]{:S(2)}, u32[]{:S(2)}) %all-to-all-start.1) | async-done | bytes 524320 | tf_op jit(solution)/shard_map/all_to_all | solution.py:38
  13.7 3.5 %all-to-all-start.2 = ((bf16[128,4,512]{2,0,1:T(8,128)(2,1)}), bf16[128,4,512]{2,0,1:T(8,128)(2,1)S(1)}, u32[]{:S(2)}, u32[]{:S(2)}) async-start(bf16[128,4,512]{2,0,1:T(8,128)(2,1)} %bitcast.94), calls=%async_computation.2 | async-start | bytes 1048576 | tf_op jit(solution)/shard_map/all_to_all | solution.py:39
  17.2 1.3 %collective-permute-start = (bf16[512,512]{1,0:T(8,128)(2,1)S(1)}, bf16[512,512]{1,0:T(8,128)(2,1)S(1)}, u32[]{:S(2)}, u32[]{:S(2)}) collective-permute-start(bf16[512,512]{1,0:T(8,128)(2,1)S(1)} %bitcast.99), channel_id=1, source_target_pairs={{0,8},{8,16},{16,24},{1,9},{9,17},{17,25},{2,10},{10,18},{18,26},{... | collective-permute-start | bytes 1572872 | tf_op jit(solution)/shard_map/ppermute | solution.py:12
  18.5 5.9 %all-to-all-done.2 = bf16[128,4,512]{2,0,1:T(8,128)(2,1)S(1)} async-done(((bf16[128,4,512]{2,0,1:T(8,128)(2,1)}), bf16[128,4,512]{2,0,1:T(8,128)(2,1)S(1)}, u32[]{:S(2)}, u32[]{:S(2)}) %all-to-all-start.2) | async-done | bytes 524320 | tf_op jit(solution)/shard_map/all_to_all | solution.py:39
  24.3 1.3 %collective-permute-start.1 = (bf16[512,512]{1,0:T(8,128)(2,1)S(1)}, bf16[512,512]{1,0:T(8,128)(2,1)}, u32[]{:S(2)}, u32[]{:S(2)}) collective-permute-start(bf16[512,512]{1,0:T(8,128)(2,1)S(1)} %bitcast.97), channel_id=1, source_target_pairs={{0,8},{8,16},{16,24},{1,9},{9,17},{17,25},{2,10},{10,18},{18,26},{... | collective-permute-start | bytes 1572872 | tf_op jit(solution)/shard_map/ppermute | solution.py:12
  25.6 0.8 copy.129
  26.5 3.5 %all-to-all-start = ((bf16[128,4,512]{2,0,1:T(8,128)(2,1)}), bf16[128,4,512]{2,0,1:T(8,128)(2,1)S(1)}, u32[]{:S(2)}, u32[]{:S(2)}) async-start(bf16[128,4,512]{2,0,1:T(8,128)(2,1)} %bitcast.96), calls=%async_computation | async-start | bytes 1048576 | tf_op jit(solution)/shard_map/all_to_all | solution.py:37
  30.1 6.4 %all-to-all-done = bf16[128,4,512]{2,0,1:T(8,128)(2,1)S(1)} async-done(((bf16[128,4,512]{2,0,1:T(8,128)(2,1)}), bf16[128,4,512]{2,0,1:T(8,128)(2,1)S(1)}, u32[]{:S(2)}, u32[]{:S(2)}) %all-to-all-start) | async-done | bytes 524320 | tf_op jit(solution)/shard_map/all_to_all | solution.py:37
  36.8 1.3 %collective-permute-start.2 = (bf16[512,512]{1,0:T(8,128)(2,1)S(1)}, bf16[512,512]{1,0:T(8,128)(2,1)}, u32[]{:S(2)}, u32[]{:S(2)}) collective-permute-start(bf16[512,512]{1,0:T(8,128)(2,1)S(1)} %collective-permute-done), channel_id=1, source_target_pairs={{0,8},{8,16},{16,24},{1,9},{9,17},{17,25},{2,10},{10,18},{18,26},{... | collective-permute-start | bytes 1572872 | tf_op jit(solution)/shard_map/ppermute | solution.py:12
  38.1 7.1 %collective-permute-done.1 = bf16[512,512]{1,0:T(8,128)(2,1)} collective-permute-done((bf16[512,512]{1,0:T(8,128)(2,1)S(1)}, bf16[512,512]{1,0:T(8,128)(2,1)}, u32[]{:S(2)}, u32[]{:S(2)}) %collective-permute-start.1) | collective-permute-done | bytes 524320 | tf_op jit(solution)/shard_map/ppermute | solution.py:12
  45.2 1.3 %collective-permute-start.3 = (bf16[512,512]{1,0:T(8,128)(2,1)}, bf16[512,512]{1,0:T(8,128)(2,1)}, u32[]{:S(2)}, u32[]{:S(2)}) collective-permute-start(bf16[512,512]{1,0:T(8,128)(2,1)} %collective-permute-done.1), channel_id=1, source_target_pairs={{0,8},{8,16},{16,24},{1,9},{9,17},{17,25},{2,10},{10,18},{18,26},{... | collective-permute-start | bytes 1572872 | tf_op jit(solution)/shard_map/ppermute | solution.py:12
  46.5 0.9 fusion.58
  47.4 1.9 %copy-done.1 = f32[4,512,512]{1,2,0:T(8,128)} copy-done((f32[4,512,512]{1,2,0:T(8,128)}, f32[4,512,512]{1,2,0:T(8,128)S(1)}, u32[]{:S(2)}) %copy-start.1) | copy-done | bytes 4194328
  49.4 0.9 fusion.60
  50.3 6.1 %collective-permute-done.2 = bf16[512,512]{1,0:T(8,128)(2,1)} collective-permute-done((bf16[512,512]{1,0:T(8,128)(2,1)S(1)}, bf16[512,512]{1,0:T(8,128)(2,1)}, u32[]{:S(2)}, u32[]{:S(2)}) %collective-permute-start.2) | collective-permute-done | bytes 524320 | tf_op jit(solution)/shard_map/ppermute | solution.py:12
  56.4 1.3 %collective-permute-start.4 = (bf16[512,512]{1,0:T(8,128)(2,1)}, bf16[512,512]{1,0:T(8,128)(2,1)S(1)}, u32[]{:S(2)}, u32[]{:S(2)}) collective-permute-start(bf16[512,512]{1,0:T(8,128)(2,1)} %collective-permute-done.2), channel_id=1, source_target_pairs={{0,8},{8,16},{16,24},{1,9},{9,17},{17,25},{2,10},{10,18},{18,26},{... | collective-permute-start | bytes 1572872 | tf_op jit(solution)/shard_map/ppermute | solution.py:12
  57.7 9.9 %collective-permute-done.3 = bf16[512,512]{1,0:T(8,128)(2,1)} collective-permute-done((bf16[512,512]{1,0:T(8,128)(2,1)}, bf16[512,512]{1,0:T(8,128)(2,1)}, u32[]{:S(2)}, u32[]{:S(2)}) %collective-permute-start.3) | collective-permute-done | bytes 524320 | tf_op jit(solution)/shard_map/ppermute | solution.py:12
  67.7 1.3 %collective-permute-start.5 = (bf16[512,512]{1,0:T(8,128)(2,1)}, bf16[512,512]{1,0:T(8,128)(2,1)}, u32[]{:S(2)}, u32[]{:S(2)}) collective-permute-start(bf16[512,512]{1,0:T(8,128)(2,1)} %collective-permute-done.3), channel_id=1, source_target_pairs={{0,8},{8,16},{16,24},{1,9},{9,17},{17,25},{2,10},{10,18},{18,26},{... | collective-permute-start | bytes 1572872 | tf_op jit(solution)/shard_map/ppermute | solution.py:12
  69.1 3.8 %fusion.70 = f32[512,4,128]{2,0,1:T(8,128)S(1)} fusion(f32[4,512,512]{1,2,0:T(8,128)} %copy-done.1, f32[4,512]{1,0:T(4,128)S(1)} %get-tuple-element.157, pred[512,512]{0,1:T(8,128)(4,1)S(1)} %iota_compare_fusion, bf16[512,4,128]{2,1,0:T(4,128)(2,1)S(1)} %reshape.86, f32[512,4]{0,1:T(4,128)S(1)} %get-tuple-element.151), kind=kOutput, calls=%fused_computation.66 | convolution fusion | flops 272891904 | bytes 6045696 | tf_op jit(solution)/shard_map/hqk,khd->qhd/dot_general | solution.py:25
  72.9 1.2 %reshape.87 = bf16[512,4,128]{2,1,0:T(4,128)(2,1)S(1)} reshape(bf16[512,512]{1,0:T(8,128)(2,1)} %copy-done.4) | data formatting | bytes 1048576 | tf_op jit(solution)/shard_map/reshape | solution.py:65
  74.0 1.2 %reshape.88 = bf16[512,4,128]{2,1,0:T(4,128)(2,1)S(1)} reshape(bf16[512,512]{1,0:T(8,128)(2,1)} %collective-permute-done.1) | data formatting | bytes 1048576 | tf_op jit(solution)/shard_map/reshape | solution.py:66
  75.2 2.9 %conditional.3 = ((f32[4,512]{1,0:T(4,128)S(1)}, f32[4,512]{1,0:T(4,128)S(1)}, f32[512,4,128]{2,0,1:T(8,128)S(1)})) conditional(s32[]{:T(128)} %convert_element_type.49, (f32[4,512]{1,0:T(4,128)S(1)}, f32[4,512]{1,0:T(4,128)S(1)}, f32[512,4,128]{2,0,1:T(8,128)S(1)}) %tuple.25, (bf16[512,4,128]{2,1,0:T(4,128)(2,1)S(1)}, ...), branch_computations={%region_2.3_spmd, %region_3.6_spmd} | conditional | flops 545789952 | bytes 16384032 | solution.py:74
  75.2 0.7 multiply_reduce_fusion
  76.0 0.7 fusion.1
  76.7 1.4 %fusion.9 = f32[512,4,128]{2,0,1:T(8,128)S(1)} fusion(f32[4,512,512]{1,2,0:T(8,128)S(1)} %get-tuple-element.144, f32[4,512]{1,0:T(4,128)S(1)} %get-tuple-element.162, f32[512,4,128]{2,0,1:T(8,128)S(1)} %get-tuple-element.65, bf16[512,4,128]{2,1,0:T(4,128)(2,1)S(1)} %get-tuple-element.124, f32[512,4]{0,1:T(4,128)S(1)} %get-tuple-element.137), kind=kOutput, calls=%fused_computation.8 | convolution fusion | flops 272105472 | bytes 6832128 | tf_op jit(solution)/shard_map/cond/branch_1_fun/hqk,khd->qhd/dot_general | solution.py:25
  78.2 5.0 %conditional.4 = ((f32[4,512]{1,0:T(4,128)S(1)}, f32[4,512]{1,0:T(4,128)S(1)}, f32[512,4,128]{2,0,1:T(8,128)S(1)})) conditional(s32[]{:T(128)} %convert_element_type.48, (f32[4,512]{1,0:T(4,128)S(1)}, f32[4,512]{1,0:T(4,128)S(1)}, f32[512,4,128]{2,0,1:T(8,128)S(1)}) %get-tuple-element.175, (bf16[512,512]{1,0:T(8,128)(2,1)}, ...), branch_computations={%region_6.7_spmd, %region_7.10_spmd} | conditional | flops 545789952 | bytes 16384032 | solution.py:74
  78.2 1.8 %multiply_reduce_fusion.1 = (f32[4,512]{1,0:T(4,128)S(1)}, f32[4,512,512]{1,2,0:T(8,128)S(1)}) fusion(bf16[512,4,128]{2,1,0:T(4,128)(2,1)S(1)} %get-tuple-element.126, bf16[512,512]{1,0:T(8,128)(2,1)} %get-tuple-element.69), kind=kOutput, calls=%fused_computation.18 | convolution fusion | flops 270530560 | bytes 5251072 | tf_op jit(solution)/shard_map/cond/branch_1_fun/qhd,khd->hqk/dot_general | solution.py:17
  80.0 0.7 fusion.19
  80.7 2.4 %fusion.27 = f32[512,4,128]{2,0,1:T(8,128)S(1)} fusion(f32[4,512,512]{1,2,0:T(8,128)S(1)} %get-tuple-element.146, f32[4,512]{1,0:T(4,128)S(1)} %get-tuple-element.168, f32[512,4,128]{2,0,1:T(8,128)S(1)} %get-tuple-element.71, f32[512,4]{0,1:T(4,128)S(1)} %get-tuple-element.139, bf16[512,512]{1,0:T(8,128)(2,1)} %get-tuple-element.72), kind=kOutput, calls=%fused_computation.25 | convolution fusion | flops 272105472 | bytes 6832128 | tf_op jit(solution)/shard_map/cond/branch_1_fun/hqk,khd->qhd/dot_general | solution.py:25
  83.1 4.8 %collective-permute-done.5 = bf16[512,512]{1,0:T(8,128)(2,1)} collective-permute-done((bf16[512,512]{1,0:T(8,128)(2,1)}, bf16[512,512]{1,0:T(8,128)(2,1)}, u32[]{:S(2)}, u32[]{:S(2)}) %collective-permute-start.5) | collective-permute-done | bytes 524320 | tf_op jit(solution)/shard_map/ppermute | solution.py:12
  87.9 3.9 %conditional.5 = ((f32[4,512]{1,0:T(4,128)S(1)}, f32[512,4,128]{2,0,1:T(8,128)S(1)})) conditional(s32[]{:T(128)} %convert_element_type.47, (f32[4,512]{1,0:T(4,128)S(1)}, f32[512,4,128]{2,0,1:T(8,128)S(1)}) %tuple.28, (bf16[512,512]{1,0:T(8,128)(2,1)S(1)}, bf16[512,4,128]{2,1,0:T(4,128)(2,1)S(1)}, f32[4,512]{1,0:T(4,128)S(1)}, ...), branch_computations={%region_10.11_spmd, %region_11.14_spmd} | conditional | flops 545789952 | bytes 16367640 | solution.py:74
  87.9 0.7 multiply_reduce_fusion.2
  88.7 0.7 fusion.39
  89.4 2.4 %fusion.47 = f32[512,4,128]{2,0,1:T(8,128)S(1)} fusion(f32[4,512,512]{1,2,0:T(8,128)S(1)} %get-tuple-element.148, f32[4,512]{1,0:T(4,128)S(1)} %get-tuple-element.142, f32[512,4,128]{2,0,1:T(8,128)S(1)} %get-tuple-element.77, f32[512,4]{0,1:T(4,128)S(1)} %get-tuple-element.141, bf16[512,512]{1,0:T(8,128)(2,1)} %get-tuple-element.78), kind=kOutput, calls=%fused_computation.44 | convolution fusion | flops 272105472 | bytes 6832128 | tf_op jit(solution)/shard_map/cond/branch_1_fun/hqk,khd->qhd/dot_general | solution.py:25
  91.9 0.3 divide_convert_fusion
  92.2 0.4 copy.60
  92.6 1.0 all_to_all.61
  93.6 3.9 %all-to-all-start.3 = ((bf16[4,128,512]{2,1,0:T(8,128)(2,1)}), bf16[4,128,512]{2,1,0:T(8,128)(2,1)S(1)}, u32[]{:S(2)}, u32[]{:S(2)}) async-start(bf16[4,128,512]{2,1,0:T(8,128)(2,1)} %all_to_all.61), calls=%async_computation.3 | async-start | bytes 1048576 | tf_op jit(solution)/shard_map/all_to_all | solution.py:78
  97.6 0.3 copy.67
  97.9 0.3 copy.68
  98.4 0.7 fusion.93
  99.0 5.0 %all-to-all-done.3 = bf16[4,128,512]{2,1,0:T(8,128)(2,1)S(1)} async-done(((bf16[4,128,512]{2,1,0:T(8,128)(2,1)}), bf16[4,128,512]{2,1,0:T(8,128)(2,1)S(1)}, u32[]{:S(2)}, u32[]{:S(2)}) %all-to-all-start.3) | async-done | bytes 524320 | tf_op jit(solution)/shard_map/all_to_all | solution.py:78
  104.2 0.3 copy.61
  104.5 2.8 %fusion.77 = bf16[128,2048]{0,1:T(8,128)(2,1)S(1)} fusion(bf16[1,128,2048]{1,2,0:T(8,128)(2,1)S(1)} %copy.67, bf16[1,128,2048]{1,2,0:T(8,128)(2,1)S(1)} %copy.68, f32[128,4,512]{0,2,1:T(8,128)S(1)} %copy.61, f32[]{:T(128)} %bitcast.20, f32[]{:T(128)} %bitcast.19, f32[]{:T(128)} %bitcast.7, f32[]{:T(128)} %bitcast.6), kind=kLoop, calls=%fused_computation.75 | loop fusion | flops 2883584 | bytes 2621456 | tf_op jit(solution)/shard_map/convert_element_type | solution.py:80
  107.4 1.0 copy.62
  (29 shorter events, 1.0 us)
Async XLA Ops:
  0.0 98.2 %copy-start = (f32[2,64]{1,0:T(2,128)S(1)}, f32[2,64]{1,0:T(2,128)}, u32[]{:S(2)}) copy-start(f32[2,64]{1,0:T(2,128)} %param.17) | copy-start | bytes 1540
  0.0 25.6 %copy-start.3 = (bf16[128,2048]{1,0:T(8,128)(2,1)S(1)}, bf16[128,2048]{1,0:T(8,128)(2,1)}, u32[]{:S(2)}) copy-start(bf16[128,2048]{1,0:T(8,128)(2,1)} %param.12) | copy-start | bytes 1572868
  1.9 11.7 %all-to-all-start.1 = ((bf16[128,4,512]{2,0,1:T(8,128)(2,1)}), bf16[128,4,512]{2,0,1:T(8,128)(2,1)S(1)}, u32[]{:S(2)}, u32[]{:S(2)}) async-start(bf16[128,4,512]{2,0,1:T(8,128)(2,1)} %bitcast.95), calls=%async_computation.1 | async-start | bytes 1048576 | tf_op jit(solution)/shard_map/all_to_all | solution.py:38
  13.7 10.7 %all-to-all-start.2 = ((bf16[128,4,512]{2,0,1:T(8,128)(2,1)}), bf16[128,4,512]{2,0,1:T(8,128)(2,1)S(1)}, u32[]{:S(2)}, u32[]{:S(2)}) async-start(bf16[128,4,512]{2,0,1:T(8,128)(2,1)} %bitcast.94), calls=%async_computation.2 | async-start | bytes 1048576 | tf_op jit(solution)/shard_map/all_to_all | solution.py:39
  17.2 19.6 %collective-permute-start = (bf16[512,512]{1,0:T(8,128)(2,1)S(1)}, bf16[512,512]{1,0:T(8,128)(2,1)S(1)}, u32[]{:S(2)}, u32[]{:S(2)}) collective-permute-start(bf16[512,512]{1,0:T(8,128)(2,1)S(1)} %bitcast.99), channel_id=1, source_target_pairs={{0,8},{8,16},{16,24},{1,9},{9,17},{17,25},{2,10},{10,18},{18,26},{... | collective-permute-start | bytes 1572872 | tf_op jit(solution)/shard_map/ppermute | solution.py:12
  24.3 20.9 %collective-permute-start.1 = (bf16[512,512]{1,0:T(8,128)(2,1)S(1)}, bf16[512,512]{1,0:T(8,128)(2,1)}, u32[]{:S(2)}, u32[]{:S(2)}) collective-permute-start(bf16[512,512]{1,0:T(8,128)(2,1)S(1)} %bitcast.97), channel_id=1, source_target_pairs={{0,8},{8,16},{16,24},{1,9},{9,17},{17,25},{2,10},{10,18},{18,26},{... | collective-permute-start | bytes 1572872 | tf_op jit(solution)/shard_map/ppermute | solution.py:12
  26.5 10.0 %all-to-all-start = ((bf16[128,4,512]{2,0,1:T(8,128)(2,1)}), bf16[128,4,512]{2,0,1:T(8,128)(2,1)S(1)}, u32[]{:S(2)}, u32[]{:S(2)}) async-start(bf16[128,4,512]{2,0,1:T(8,128)(2,1)} %bitcast.96), calls=%async_computation | async-start | bytes 1048576 | tf_op jit(solution)/shard_map/all_to_all | solution.py:37
  36.8 13.5 %copy-start.4 = (bf16[512,512]{1,0:T(8,128)(2,1)}, bf16[512,512]{1,0:T(8,128)(2,1)S(1)}, u32[]{:S(2)}) copy-start(bf16[512,512]{1,0:T(8,128)(2,1)S(1)} %collective-permute-done) | copy-start | bytes 1572868
  36.8 19.6 %collective-permute-start.2 = (bf16[512,512]{1,0:T(8,128)(2,1)S(1)}, bf16[512,512]{1,0:T(8,128)(2,1)}, u32[]{:S(2)}, u32[]{:S(2)}) collective-permute-start(bf16[512,512]{1,0:T(8,128)(2,1)S(1)} %collective-permute-done), channel_id=1, source_target_pairs={{0,8},{8,16},{16,24},{1,9},{9,17},{17,25},{2,10},{10,18},{18,26},{... | collective-permute-start | bytes 1572872 | tf_op jit(solution)/shard_map/ppermute | solution.py:12
  45.2 22.5 %collective-permute-start.3 = (bf16[512,512]{1,0:T(8,128)(2,1)}, bf16[512,512]{1,0:T(8,128)(2,1)}, u32[]{:S(2)}, u32[]{:S(2)}) collective-permute-start(bf16[512,512]{1,0:T(8,128)(2,1)} %collective-permute-done.1), channel_id=1, source_target_pairs={{0,8},{8,16},{16,24},{1,9},{9,17},{17,25},{2,10},{10,18},{18,26},{... | collective-permute-start | bytes 1572872 | tf_op jit(solution)/shard_map/ppermute | solution.py:12
  47.4 1.9 %copy-start.1 = (f32[4,512,512]{1,2,0:T(8,128)}, f32[4,512,512]{1,2,0:T(8,128)S(1)}, u32[]{:S(2)}) copy-start(f32[4,512,512]{1,2,0:T(8,128)S(1)} %get-tuple-element.158) | copy-start | bytes 12582916
  56.4 26.7 %collective-permute-start.4 = (bf16[512,512]{1,0:T(8,128)(2,1)}, bf16[512,512]{1,0:T(8,128)(2,1)S(1)}, u32[]{:S(2)}, u32[]{:S(2)}) collective-permute-start(bf16[512,512]{1,0:T(8,128)(2,1)} %collective-permute-done.2), channel_id=1, source_target_pairs={{0,8},{8,16},{16,24},{1,9},{9,17},{17,25},{2,10},{10,18},{18,26},{... | collective-permute-start | bytes 1572872 | tf_op jit(solution)/shard_map/ppermute | solution.py:12
  67.7 20.3 %collective-permute-start.5 = (bf16[512,512]{1,0:T(8,128)(2,1)}, bf16[512,512]{1,0:T(8,128)(2,1)}, u32[]{:S(2)}, u32[]{:S(2)}) collective-permute-start(bf16[512,512]{1,0:T(8,128)(2,1)} %collective-permute-done.3), channel_id=1, source_target_pairs={{0,8},{8,16},{16,24},{1,9},{9,17},{17,25},{2,10},{10,18},{18,26},{... | collective-permute-start | bytes 1572872 | tf_op jit(solution)/shard_map/ppermute | solution.py:12
  91.8 5.7 %copy-start.2 = (bf16[2,128,2048]{2,1,0:T(8,128)(2,1)S(1)}, bf16[2,128,2048]{2,1,0:T(8,128)(2,1)}, u32[]{:S(2)}) copy-start(bf16[2,128,2048]{2,1,0:T(8,128)(2,1)} %param.15) | copy-start | bytes 3145732
  91.9 6.3 %copy-start.5 = (s32[2]{0:T(128)S(1)}, s32[2]{0:T(128)}, u32[]{:S(2)}) copy-start(s32[2]{0:T(128)} %param.16) | copy-start | bytes 28
  93.6 10.4 %all-to-all-start.3 = ((bf16[4,128,512]{2,1,0:T(8,128)(2,1)}), bf16[4,128,512]{2,1,0:T(8,128)(2,1)S(1)}, u32[]{:S(2)}, u32[]{:S(2)}) async-start(bf16[4,128,512]{2,1,0:T(8,128)(2,1)} %all_to_all.61), calls=%async_computation.3 | async-start | bytes 1048576 | tf_op jit(solution)/shard_map/all_to_all | solution.py:78
where the time goes:
time: 109 us; the launch traced here: 108 us
  waiting for transfers between devices  51.5 us (47%)
  starting transfers between devices  22.2 us (20%)
  matrix products  14.4 us (13%)
  local copies, waits for them, and re-layouts  13.4 us (12%)
  other arithmetic  6.49 us (6%)
    ppermute x6, waiting for transfers between devices, from_behind(): return lax.ppermute(block, axis, route)  28 us
    dot_general x4, matrix products, block_update(): jnp.einsum('hqk,khd->qhd', weights, value_heads, preferred_element_type=j...  10.1 us
    ppermute x6, starting transfers between devices, from_behind(): return lax.ppermute(block, axis, route)  7.71 us
    all_to_all x1, waiting for transfers between devices, shards(): lax.all_to_all(queries, 'uly', split_axis=1, concat_axis=0, tiled=True)  6.45 us
    all_to_all x1, waiting for transfers between devices, shards(): lax.all_to_all(keys, 'uly', split_axis=1, concat_axis=0, tiled=True)  6.15 us
    all_to_all x1, waiting for transfers between devices, shards(): lax.all_to_all(values, 'uly', split_axis=1, concat_axis=0, tiled=True)  5.88 us
    all_to_all x1, waiting for transfers between devices, shards(): lax.all_to_all(attended, 'uly', split_axis=0, concat_axis=1, tiled=True)  5.04 us
    dot_general x4, matrix products, block_update(): jnp.einsum('qhd,khd->hqk', query_heads, key_heads, preferred_element_type...  4.16 us
  transfers between devices with their start and end apart: 10, of which 8 were waited for; matrix products, arithmetic and copies ran while one was open for 19% of the time, Pallas kernels for 0%

commit v1 on v0

--- a/solution.py
+++ b/solution.py
@@ -4,6 +4,12 @@
 from jax.sharding import PartitionSpec as P
 
 HEAD_DIM = 128
+
+
+def swap_blocks(shard, axis, split, join):
+    parts = jnp.split(shard, lax.axis_size(axis), axis=split)
+    arrived = lax.all_to_all(jnp.stack(parts), axis, 0, 0)
+    return jnp.concatenate(arrived, axis=join)
 
 
 def from_behind(block, axis, distance):
@@ -34,7 +40,7 @@
     features = queries.shape[1]
     local_heads = features // n_uly // HEAD_DIM
     query_rows, key_rows, value_rows = (
-        lax.all_to_all(queries, "uly", split_axis=1, concat_axis=0, tiled=True),
+        swap_blocks(queries, "uly", 1, 0),
         lax.all_to_all(keys, "uly", split_axis=1, concat_axis=0, tiled=True),
         lax.all_to_all(values, "uly", split_axis=1, concat_axis=0, tiled=True),
     )

time: 109 us -> 109 us (level)
  waiting for transfers between devices: 51.5 us -> 49.6 us
  transfers between devices with their start and end apart: 10 -> 10, of which waited for: 8 -> 8; matrix products, arithmetic and copies ran while one was open for 19% -> 21% of each run, Pallas kernels for 0% -> 0%
where the time goes in v1:
time: 109 us; the launch traced here: 108 us
  waiting for transfers between devices  49.6 us (46%)
  starting transfers between devices  22.2 us (20%)
  matrix products  15.4 us (14%)
  local copies, waits for them, and re-layouts  13.4 us (12%)
  other arithmetic  7.4 us (7%)
    ppermute x6, waiting for transfers between devices, from_behind(): return lax.ppermute(block, axis, route)  27 us
    dot_general x4, matrix products, block_update(): jnp.einsum('hqk,khd->qhd', weights, value_heads, preferred_element_type=j...  10.1 us
    ppermute x6, starting transfers between devices, from_behind(): return lax.ppermute(block, axis, route)  7.71 us
    all_to_all x1, waiting for transfers between devices, shards(): lax.all_to_all(keys, 'uly', split_axis=1, concat_axis=0, tiled=True)  6.15 us
    all_to_all x1, waiting for transfers between devices, shards(): lax.all_to_all(values, 'uly', split_axis=1, concat_axis=0, tiled=True)  5.88 us
    all_to_all x1, waiting for transfers between devices, swap_blocks(): arrived = lax.all_to_all(jnp.stack(parts), axis, 0, 0)  5.53 us
    dot_general x4, matrix products, block_update(): jnp.einsum('qhd,khd->hqk', query_heads, key_heads, preferred_element_type...  5.19 us
    all_to_all x1, waiting for transfers between devices, shards(): lax.all_to_all(attended, 'uly', split_axis=0, concat_axis=1, tiled=True)  5.08 us
  transfers between devices with their start and end apart: 10, of which 8 were waited for; matrix products, arithmetic and copies ran while one was open for 21% of the time, Pallas kernels for 0%

profile of v1, /device:TPU:24, one launch (start us, length us, event | category | flops | bytes accessed | tf_op | source)
XLA Modules:
  0.0 108.4 jit_solution(8069524321338366013)
XLA Ops:
  0.0 1.9 %copy.124 = bf16[16,4,8,512]{3,2,0,1:T(8,128)(2,1)} copy(bf16[16,4,8,512]{3,2,1,0:T(8,128)(2,1)} %bitcast.104) | data formatting | bytes 1048576 | tf_op jit(solution)/shard_map/all_to_all | solution.py:44
  1.9 3.7 %all-to-all-start.1 = ((bf16[128,4,512]{2,0,1:T(8,128)(2,1)}), bf16[128,4,512]{2,0,1:T(8,128)(2,1)S(1)}, u32[]{:S(2)}, u32[]{:S(2)}) async-start(bf16[128,4,512]{2,0,1:T(8,128)(2,1)} %bitcast.99), calls=%async_computation.1 | async-start | bytes 1048576 | tf_op jit(solution)/shard_map/all_to_all | solution.py:44
  5.7 1.9 %copy.123 = bf16[16,4,8,512]{3,2,0,1:T(8,128)(2,1)} copy(bf16[16,4,8,512]{3,2,1,0:T(8,128)(2,1)} %bitcast.105) | data formatting | bytes 1048576 | tf_op jit(solution)/shard_map/all_to_all | solution.py:45
  7.5 6.1 %all-to-all-done.1 = bf16[128,4,512]{2,0,1:T(8,128)(2,1)S(1)} async-done(((bf16[128,4,512]{2,0,1:T(8,128)(2,1)}), bf16[128,4,512]{2,0,1:T(8,128)(2,1)S(1)}, u32[]{:S(2)}, u32[]{:S(2)}) %all-to-all-start.1) | async-done | bytes 524320 | tf_op jit(solution)/shard_map/all_to_all | solution.py:44
  13.7 3.5 %all-to-all-start.2 = ((bf16[128,4,512]{2,0,1:T(8,128)(2,1)}), bf16[128,4,512]{2,0,1:T(8,128)(2,1)S(1)}, u32[]{:S(2)}, u32[]{:S(2)}) async-start(bf16[128,4,512]{2,0,1:T(8,128)(2,1)} %bitcast.98), calls=%async_computation.2 | async-start | bytes 1048576 | tf_op jit(solution)/shard_map/all_to_all | solution.py:45
  17.2 1.3 %collective-permute-start = (bf16[512,512]{1,0:T(8,128)(2,1)S(1)}, bf16[512,512]{1,0:T(8,128)(2,1)S(1)}, u32[]{:S(2)}, u32[]{:S(2)}) collective-permute-start(bf16[512,512]{1,0:T(8,128)(2,1)S(1)} %bitcast.102), channel_id=1, source_target_pairs={{0,8},{8,16},{16,24},{1,9},{9,17},{17,25},{2,10},{10,18},{18,26},{... | collective-permute-start | bytes 1572872 | tf_op jit(solution)/shard_map/ppermute | solution.py:18
  18.5 5.9 %all-to-all-done.2 = bf16[128,4,512]{2,0,1:T(8,128)(2,1)S(1)} async-done(((bf16[128,4,512]{2,0,1:T(8,128)(2,1)}), bf16[128,4,512]{2,0,1:T(8,128)(2,1)S(1)}, u32[]{:S(2)}, u32[]{:S(2)}) %all-to-all-start.2) | async-done | bytes 524320 | tf_op jit(solution)/shard_map/all_to_all | solution.py:45
  24.3 1.3 %collective-permute-start.1 = (bf16[512,512]{1,0:T(8,128)(2,1)S(1)}, bf16[512,512]{1,0:T(8,128)(2,1)}, u32[]{:S(2)}, u32[]{:S(2)}) collective-permute-start(bf16[512,512]{1,0:T(8,128)(2,1)S(1)} %bitcast.100), channel_id=1, source_target_pairs={{0,8},{8,16},{16,24},{1,9},{9,17},{17,25},{2,10},{10,18},{18,26},{... | collective-permute-start | bytes 1572872 | tf_op jit(solution)/shard_map/ppermute | solution.py:18
  25.7 0.9 pad_maximum_fusion
  26.5 3.5 %all-to-all-start = ((bf16[4,128,512]{2,1,0:T(8,128)(2,1)}), bf16[4,128,512]{2,1,0:T(8,128)(2,1)S(1)}, u32[]{:S(2)}, u32[]{:S(2)}) async-start(bf16[4,128,512]{2,1,0:T(8,128)(2,1)} %pad_maximum_fusion), calls=%async_computation | async-start | bytes 1048576 | tf_op jit(solution)/shard_map/all_to_all | solution.py:11
  30.1 0.9 reshape.77
  31.0 5.5 %all-to-all-done = bf16[4,128,512]{2,1,0:T(8,128)(2,1)S(1)} async-done(((bf16[4,128,512]{2,1,0:T(8,128)(2,1)}), bf16[4,128,512]{2,1,0:T(8,128)(2,1)S(1)}, u32[]{:S(2)}, u32[]{:S(2)}) %all-to-all-start) | async-done | bytes 524320 | tf_op jit(solution)/shard_map/all_to_all | solution.py:11
  36.7 1.3 %collective-permute-start.2 = (bf16[512,512]{1,0:T(8,128)(2,1)S(1)}, bf16[512,512]{1,0:T(8,128)(2,1)}, u32[]{:S(2)}, u32[]{:S(2)}) collective-permute-start(bf16[512,512]{1,0:T(8,128)(2,1)S(1)} %collective-permute-done), channel_id=1, source_target_pairs={{0,8},{8,16},{16,24},{1,9},{9,17},{17,25},{2,10},{10,18},{18,26},{... | collective-permute-start | bytes 1572872 | tf_op jit(solution)/shard_map/ppermute | solution.py:18
  38.0 7.2 %collective-permute-done.1 = bf16[512,512]{1,0:T(8,128)(2,1)} collective-permute-done((bf16[512,512]{1,0:T(8,128)(2,1)S(1)}, bf16[512,512]{1,0:T(8,128)(2,1)}, u32[]{:S(2)}, u32[]{:S(2)}) %collective-permute-start.1) | collective-permute-done | bytes 524320 | tf_op jit(solution)/shard_map/ppermute | solution.py:18
  45.2 1.3 %collective-permute-start.3 = (bf16[512,512]{1,0:T(8,128)(2,1)}, bf16[512,512]{1,0:T(8,128)(2,1)}, u32[]{:S(2)}, u32[]{:S(2)}) collective-permute-start(bf16[512,512]{1,0:T(8,128)(2,1)} %collective-permute-done.1), channel_id=1, source_target_pairs={{0,8},{8,16},{16,24},{1,9},{9,17},{17,25},{2,10},{10,18},{18,26},{... | collective-permute-start | bytes 1572872 | tf_op jit(solution)/shard_map/ppermute | solution.py:18
  46.5 2.0 %fusion.58 = (f32[4,512]{1,0:T(4,128)S(1)}, f32[4,512,512]{1,2,0:T(8,128)S(1)}) fusion(pred[512,512]{0,1:T(8,128)(4,1)S(1)} %iota_compare_fusion, bf16[512,4,128]{2,1,0:T(4,128)(2,1)} %reshape.77, bf16[512,4,128]{2,1,0:T(4,128)(2,1)S(1)} %reshape_reshape.3), kind=kOutput, calls=%fused_computation.57 | convolution fusion | flops 271579136 | bytes 5513216 | tf_op jit(solution)/shard_map/qhd,khd->hqk/dot_general | solution.py:23
  48.5 1.9 %copy-done.1 = f32[4,512,512]{1,2,0:T(8,128)} copy-done((f32[4,512,512]{1,2,0:T(8,128)}, f32[4,512,512]{1,2,0:T(8,128)S(1)}, u32[]{:S(2)}) %copy-start.1) | copy-done | bytes 4194328
  50.4 0.9 fusion.60
  51.3 5.1 %collective-permute-done.2 = bf16[512,512]{1,0:T(8,128)(2,1)} collective-permute-done((bf16[512,512]{1,0:T(8,128)(2,1)S(1)}, bf16[512,512]{1,0:T(8,128)(2,1)}, u32[]{:S(2)}, u32[]{:S(2)}) %collective-permute-start.2) | collective-permute-done | bytes 524320 | tf_op jit(solution)/shard_map/ppermute | solution.py:18
  56.4 1.3 %collective-permute-start.4 = (bf16[512,512]{1,0:T(8,128)(2,1)}, bf16[512,512]{1,0:T(8,128)(2,1)S(1)}, u32[]{:S(2)}, u32[]{:S(2)}) collective-permute-start(bf16[512,512]{1,0:T(8,128)(2,1)} %collective-permute-done.2), channel_id=1, source_target_pairs={{0,8},{8,16},{16,24},{1,9},{9,17},{17,25},{2,10},{10,18},{18,26},{... | collective-permute-start | bytes 1572872 | tf_op jit(solution)/shard_map/ppermute | solution.py:18
  57.7 9.9 %collective-permute-done.3 = bf16[512,512]{1,0:T(8,128)(2,1)} collective-permute-done((bf16[512,512]{1,0:T(8,128)(2,1)}, bf16[512,512]{1,0:T(8,128)(2,1)}, u32[]{:S(2)}, u32[]{:S(2)}) %collective-permute-start.3) | collective-permute-done | bytes 524320 | tf_op jit(solution)/shard_map/ppermute | solution.py:18
  67.7 1.3 %collective-permute-start.5 = (bf16[512,512]{1,0:T(8,128)(2,1)}, bf16[512,512]{1,0:T(8,128)(2,1)}, u32[]{:S(2)}, u32[]{:S(2)}) collective-permute-start(bf16[512,512]{1,0:T(8,128)(2,1)} %collective-permute-done.3), channel_id=1, source_target_pairs={{0,8},{8,16},{16,24},{1,9},{9,17},{17,25},{2,10},{10,18},{18,26},{... | collective-permute-start | bytes 1572872 | tf_op jit(solution)/shard_map/ppermute | solution.py:18
  69.1 3.8 %fusion.70 = f32[512,4,128]{2,0,1:T(8,128)S(1)} fusion(f32[4,512,512]{1,2,0:T(8,128)} %copy-done.1, f32[4,512]{1,0:T(4,128)S(1)} %get-tuple-element.161, pred[512,512]{0,1:T(8,128)(4,1)S(1)} %iota_compare_fusion, bf16[512,4,128]{2,1,0:T(4,128)(2,1)S(1)} %reshape.78, f32[512,4]{0,1:T(4,128)S(1)} %get-tuple-element.155), kind=kOutput, calls=%fused_computation.66 | convolution fusion | flops 272891904 | bytes 6045696 | tf_op jit(solution)/shard_map/hqk,khd->qhd/dot_general | solution.py:31
  72.9 1.2 %reshape.79 = bf16[512,4,128]{2,1,0:T(4,128)(2,1)S(1)} reshape(bf16[512,512]{1,0:T(8,128)(2,1)} %copy-done.4) | data formatting | bytes 1048576 | tf_op jit(solution)/shard_map/reshape | solution.py:71
  74.0 1.2 %reshape.80 = bf16[512,4,128]{2,1,0:T(4,128)(2,1)S(1)} reshape(bf16[512,512]{1,0:T(8,128)(2,1)} %collective-permute-done.1) | data formatting | bytes 1048576 | tf_op jit(solution)/shard_map/reshape | solution.py:72
  75.2 2.9 %conditional.3 = ((f32[4,512]{1,0:T(4,128)S(1)}, f32[4,512]{1,0:T(4,128)S(1)}, f32[512,4,128]{2,0,1:T(8,128)S(1)})) conditional(s32[]{:T(128)} %convert_element_type.49, (f32[4,512]{1,0:T(4,128)S(1)}, f32[4,512]{1,0:T(4,128)S(1)}, f32[512,4,128]{2,0,1:T(8,128)S(1)}) %tuple.25, (bf16[512,4,128]{2,1,0:T(4,128)(2,1)S(1)}, ...), branch_computations={%region_2.3_spmd, %region_3.6_spmd} | conditional | flops 545789952 | bytes 16384032 | solution.py:80
  75.2 0.7 multiply_reduce_fusion
  76.0 0.7 fusion.1
  76.7 1.4 %fusion.9 = f32[512,4,128]{2,0,1:T(8,128)S(1)} fusion(f32[4,512,512]{1,2,0:T(8,128)S(1)} %get-tuple-element.144, f32[4,512]{1,0:T(4,128)S(1)} %get-tuple-element.166, f32[512,4,128]{2,0,1:T(8,128)S(1)} %get-tuple-element.65, bf16[512,4,128]{2,1,0:T(4,128)(2,1)S(1)} %get-tuple-element.124, f32[512,4]{0,1:T(4,128)S(1)} %get-tuple-element.137), kind=kOutput, calls=%fused_computation.8 | convolution fusion | flops 272105472 | bytes 6832128 | tf_op jit(solution)/shard_map/cond/branch_1_fun/hqk,khd->qhd/dot_general | solution.py:31
  78.1 5.0 %conditional.4 = ((f32[4,512]{1,0:T(4,128)S(1)}, f32[4,512]{1,0:T(4,128)S(1)}, f32[512,4,128]{2,0,1:T(8,128)S(1)})) conditional(s32[]{:T(128)} %convert_element_type.48, (f32[4,512]{1,0:T(4,128)S(1)}, f32[4,512]{1,0:T(4,128)S(1)}, f32[512,4,128]{2,0,1:T(8,128)S(1)}) %get-tuple-element.179, (bf16[512,512]{1,0:T(8,128)(2,1)}, ...), branch_computations={%region_6.7_spmd, %region_7.10_spmd} | conditional | flops 545789952 | bytes 16384032 | solution.py:80
  78.2 1.8 %multiply_reduce_fusion.1 = (f32[4,512]{1,0:T(4,128)S(1)}, f32[4,512,512]{1,2,0:T(8,128)S(1)}) fusion(bf16[512,4,128]{2,1,0:T(4,128)(2,1)S(1)} %get-tuple-element.126, bf16[512,512]{1,0:T(8,128)(2,1)} %get-tuple-element.69), kind=kOutput, calls=%fused_computation.18 | convolution fusion | flops 270530560 | bytes 5251072 | tf_op jit(solution)/shard_map/cond/branch_1_fun/qhd,khd->hqk/dot_general | solution.py:23
  80.0 0.7 fusion.19
  80.7 2.4 %fusion.27 = f32[512,4,128]{2,0,1:T(8,128)S(1)} fusion(f32[4,512,512]{1,2,0:T(8,128)S(1)} %get-tuple-element.146, f32[4,512]{1,0:T(4,128)S(1)} %get-tuple-element.172, f32[512,4,128]{2,0,1:T(8,128)S(1)} %get-tuple-element.71, f32[512,4]{0,1:T(4,128)S(1)} %get-tuple-element.139, bf16[512,512]{1,0:T(8,128)(2,1)} %get-tuple-element.72), kind=kOutput, calls=%fused_computation.25 | convolution fusion | flops 272105472 | bytes 6832128 | tf_op jit(solution)/shard_map/cond/branch_1_fun/hqk,khd->qhd/dot_general | solution.py:31
  83.1 4.8 %collective-permute-done.5 = bf16[512,512]{1,0:T(8,128)(2,1)} collective-permute-done((bf16[512,512]{1,0:T(8,128)(2,1)}, bf16[512,512]{1,0:T(8,128)(2,1)}, u32[]{:S(2)}, u32[]{:S(2)}) %collective-permute-start.5) | collective-permute-done | bytes 524320 | tf_op jit(solution)/shard_map/ppermute | solution.py:18
  87.9 3.9 %conditional.5 = ((f32[4,512]{1,0:T(4,128)S(1)}, f32[512,4,128]{2,0,1:T(8,128)S(1)})) conditional(s32[]{:T(128)} %convert_element_type.47, (f32[4,512]{1,0:T(4,128)S(1)}, f32[512,4,128]{2,0,1:T(8,128)S(1)}) %tuple.28, (bf16[512,512]{1,0:T(8,128)(2,1)S(1)}, bf16[512,4,128]{2,1,0:T(4,128)(2,1)S(1)}, f32[4,512]{1,0:T(4,128)S(1)}, ...), branch_computations={%region_10.11_spmd, %region_11.14_spmd} | conditional | flops 545789952 | bytes 16367640 | solution.py:80
  87.9 0.7 multiply_reduce_fusion.2
  88.7 0.7 fusion.39
  89.4 2.4 %fusion.47 = f32[512,4,128]{2,0,1:T(8,128)S(1)} fusion(f32[4,512,512]{1,2,0:T(8,128)S(1)} %get-tuple-element.148, f32[4,512]{1,0:T(4,128)S(1)} %get-tuple-element.142, f32[512,4,128]{2,0,1:T(8,128)S(1)} %get-tuple-element.77, f32[512,4]{0,1:T(4,128)S(1)} %get-tuple-element.141, bf16[512,512]{1,0:T(8,128)(2,1)} %get-tuple-element.78), kind=kOutput, calls=%fused_computation.44 | convolution fusion | flops 272105472 | bytes 6832128 | tf_op jit(solution)/shard_map/cond/branch_1_fun/hqk,khd->qhd/dot_general | solution.py:31
  91.9 0.3 divide_convert_fusion
  92.2 0.4 copy.58
  92.6 1.0 all_to_all.50
  93.6 3.9 %all-to-all-start.3 = ((bf16[4,128,512]{2,1,0:T(8,128)(2,1)}), bf16[4,128,512]{2,1,0:T(8,128)(2,1)S(1)}, u32[]{:S(2)}, u32[]{:S(2)}) async-start(bf16[4,128,512]{2,1,0:T(8,128)(2,1)} %all_to_all.50), calls=%async_computation.3 | async-start | bytes 1048576 | tf_op jit(solution)/shard_map/all_to_all | solution.py:84
  97.9 0.3 copy.66
  98.4 0.6 fusion.93
  99.0 5.1 %all-to-all-done.3 = bf16[4,128,512]{2,1,0:T(8,128)(2,1)S(1)} async-done(((bf16[4,128,512]{2,1,0:T(8,128)(2,1)}), bf16[4,128,512]{2,1,0:T(8,128)(2,1)S(1)}, u32[]{:S(2)}, u32[]{:S(2)}) %all-to-all-start.3) | async-done | bytes 524320 | tf_op jit(solution)/shard_map/all_to_all | solution.py:84
  104.2 0.3 copy.59
  104.5 2.9 %fusion.77 = bf16[128,2048]{0,1:T(8,128)(2,1)S(1)} fusion(bf16[1,128,2048]{1,2,0:T(8,128)(2,1)S(1)} %copy.65, bf16[1,128,2048]{1,2,0:T(8,128)(2,1)S(1)} %copy.66, f32[128,4,512]{0,2,1:T(8,128)S(1)} %copy.59, f32[]{:T(128)} %bitcast.23, f32[]{:T(128)} %bitcast.22, f32[]{:T(128)} %bitcast.7, f32[]{:T(128)} %bitcast.6), kind=kLoop, calls=%fused_computation.75 | loop fusion | flops 2883584 | bytes 2621456 | tf_op jit(solution)/shard_map/convert_element_type | solution.py:86
  107.4 1.0 copy.60
  (30 shorter events, 1.2 us)
Async XLA Ops:
  0.0 98.2 %copy-start = (f32[2,64]{1,0:T(2,128)S(1)}, f32[2,64]{1,0:T(2,128)}, u32[]{:S(2)}) copy-start(f32[2,64]{1,0:T(2,128)} %param.17) | copy-start | bytes 1540
  0.0 25.6 %copy-start.3 = (bf16[128,2048]{1,0:T(8,128)(2,1)S(1)}, bf16[128,2048]{1,0:T(8,128)(2,1)}, u32[]{:S(2)}) copy-start(bf16[128,2048]{1,0:T(8,128)(2,1)} %param.12) | copy-start | bytes 1572868
  1.9 11.7 %all-to-all-start.1 = ((bf16[128,4,512]{2,0,1:T(8,128)(2,1)}), bf16[128,4,512]{2,0,1:T(8,128)(2,1)S(1)}, u32[]{:S(2)}, u32[]{:S(2)}) async-start(bf16[128,4,512]{2,0,1:T(8,128)(2,1)} %bitcast.99), calls=%async_computation.1 | async-start | bytes 1048576 | tf_op jit(solution)/shard_map/all_to_all | solution.py:44
  13.7 10.7 %all-to-all-start.2 = ((bf16[128,4,512]{2,0,1:T(8,128)(2,1)}), bf16[128,4,512]{2,0,1:T(8,128)(2,1)S(1)}, u32[]{:S(2)}, u32[]{:S(2)}) async-start(bf16[128,4,512]{2,0,1:T(8,128)(2,1)} %bitcast.98), calls=%async_computation.2 | async-start | bytes 1048576 | tf_op jit(solution)/shard_map/all_to_all | solution.py:45
  17.2 19.5 %collective-permute-start = (bf16[512,512]{1,0:T(8,128)(2,1)S(1)}, bf16[512,512]{1,0:T(8,128)(2,1)S(1)}, u32[]{:S(2)}, u32[]{:S(2)}) collective-permute-start(bf16[512,512]{1,0:T(8,128)(2,1)S(1)} %bitcast.102), channel_id=1, source_target_pairs={{0,8},{8,16},{16,24},{1,9},{9,17},{17,25},{2,10},{10,18},{18,26},{... | collective-permute-start | bytes 1572872 | tf_op jit(solution)/shard_map/ppermute | solution.py:18
  24.3 20.9 %collective-permute-start.1 = (bf16[512,512]{1,0:T(8,128)(2,1)S(1)}, bf16[512,512]{1,0:T(8,128)(2,1)}, u32[]{:S(2)}, u32[]{:S(2)}) collective-permute-start(bf16[512,512]{1,0:T(8,128)(2,1)S(1)} %bitcast.100), channel_id=1, source_target_pairs={{0,8},{8,16},{16,24},{1,9},{9,17},{17,25},{2,10},{10,18},{18,26},{... | collective-permute-start | bytes 1572872 | tf_op jit(solution)/shard_map/ppermute | solution.py:18
  26.5 10.0 %all-to-all-start = ((bf16[4,128,512]{2,1,0:T(8,128)(2,1)}), bf16[4,128,512]{2,1,0:T(8,128)(2,1)S(1)}, u32[]{:S(2)}, u32[]{:S(2)}) async-start(bf16[4,128,512]{2,1,0:T(8,128)(2,1)} %pad_maximum_fusion), calls=%async_computation | async-start | bytes 1048576 | tf_op jit(solution)/shard_map/all_to_all | solution.py:11
  36.7 14.6 %copy-start.4 = (bf16[512,512]{1,0:T(8,128)(2,1)}, bf16[512,512]{1,0:T(8,128)(2,1)S(1)}, u32[]{:S(2)}) copy-start(bf16[512,512]{1,0:T(8,128)(2,1)S(1)} %collective-permute-done) | copy-start | bytes 1572868
  36.7 19.7 %collective-permute-start.2 = (bf16[512,512]{1,0:T(8,128)(2,1)S(1)}, bf16[512,512]{1,0:T(8,128)(2,1)}, u32[]{:S(2)}, u32[]{:S(2)}) collective-permute-start(bf16[512,512]{1,0:T(8,128)(2,1)S(1)} %collective-permute-done), channel_id=1, source_target_pairs={{0,8},{8,16},{16,24},{1,9},{9,17},{17,25},{2,10},{10,18},{18,26},{... | collective-permute-start | bytes 1572872 | tf_op jit(solution)/shard_map/ppermute | solution.py:18
  45.2 22.5 %collective-permute-start.3 = (bf16[512,512]{1,0:T(8,128)(2,1)}, bf16[512,512]{1,0:T(8,128)(2,1)}, u32[]{:S(2)}, u32[]{:S(2)}) collective-permute-start(bf16[512,512]{1,0:T(8,128)(2,1)} %collective-permute-done.1), channel_id=1, source_target_pairs={{0,8},{8,16},{16,24},{1,9},{9,17},{17,25},{2,10},{10,18},{18,26},{... | collective-permute-start | bytes 1572872 | tf_op jit(solution)/shard_map/ppermute | solution.py:18
  48.5 2.0 %copy-start.1 = (f32[4,512,512]{1,2,0:T(8,128)}, f32[4,512,512]{1,2,0:T(8,128)S(1)}, u32[]{:S(2)}) copy-start(f32[4,512,512]{1,2,0:T(8,128)S(1)} %get-tuple-element.162) | copy-start | bytes 12582916
  56.4 26.7 %collective-permute-start.4 = (bf16[512,512]{1,0:T(8,128)(2,1)}, bf16[512,512]{1,0:T(8,128)(2,1)S(1)}, u32[]{:S(2)}, u32[]{:S(2)}) collective-permute-start(bf16[512,512]{1,0:T(8,128)(2,1)} %collective-permute-done.2), channel_id=1, source_target_pairs={{0,8},{8,16},{16,24},{1,9},{9,17},{17,25},{2,10},{10,18},{18,26},{... | collective-permute-start | bytes 1572872 | tf_op jit(solution)/shard_map/ppermute | solution.py:18
  67.7 20.3 %collective-permute-start.5 = (bf16[512,512]{1,0:T(8,128)(2,1)}, bf16[512,512]{1,0:T(8,128)(2,1)}, u32[]{:S(2)}, u32[]{:S(2)}) collective-permute-start(bf16[512,512]{1,0:T(8,128)(2,1)} %collective-permute-done.3), channel_id=1, source_target_pairs={{0,8},{8,16},{16,24},{1,9},{9,17},{17,25},{2,10},{10,18},{18,26},{... | collective-permute-start | bytes 1572872 | tf_op jit(solution)/shard_map/ppermute | solution.py:18
  91.8 5.7 %copy-start.2 = (bf16[2,128,2048]{2,1,0:T(8,128)(2,1)S(1)}, bf16[2,128,2048]{2,1,0:T(8,128)(2,1)}, u32[]{:S(2)}) copy-start(bf16[2,128,2048]{2,1,0:T(8,128)(2,1)} %param.15) | copy-start | bytes 3145732
  91.9 6.3 %copy-start.5 = (s32[2]{0:T(128)S(1)}, s32[2]{0:T(128)}, u32[]{:S(2)}) copy-start(s32[2]{0:T(128)} %param.16) | copy-start | bytes 28
  93.6 10.4 %all-to-all-start.3 = ((bf16[4,128,512]{2,1,0:T(8,128)(2,1)}), bf16[4,128,512]{2,1,0:T(8,128)(2,1)S(1)}, u32[]{:S(2)}, u32[]{:S(2)}) async-start(bf16[4,128,512]{2,1,0:T(8,128)(2,1)} %all_to_all.50), calls=%async_computation.3 | async-start | bytes 1048576 | tf_op jit(solution)/shard_map/all_to_all | solution.py:84
